TPU v7x, 32 devices: a 4x4x1 block of a 4x4x8 slice. The times are simulated.
32 devices in a mesh: dp: 1 (over z), pp: 4 (over y), tp: 8 (over x, core).
Axes of the slice: x: 4, y: 4, z: 1, core: 2. Of those that a mesh axis runs over, the one named last changes fastest.
The devices are a block of a 4x4x8 slice.
Arguments:
- x_in: bfloat16 [16, 64, 3072], P('dp', 'tp')
- ln_gain: bfloat16 [2, 4, 3072], P(None, 'pp')
- w_in: bfloat16 [2, 4, 3072, 8192], P(None, 'pp', None, 'tp')
- w_out: bfloat16 [2, 4, 8192, 3072], P(None, 'pp', 'tp')
Outputs:
- output: bfloat16 [16, 64, 3072], P(('dp', 'pp'), 'tp')
All inputs are finite; a program needn't handle non-finite values.
Results may differ from a plain program's by a relative error of at most 0.02.
Values are sent between devices in bfloat16 or wider.
A program may use at most 768 MiB of HBM per device.

v0:
```python
import jax
import jax.numpy as jnp
from jax import lax
from jax.sharding import PartitionSpec as P

NORM_EPS = 1e-5


def layer_norm(resid, gain_vec):
    resid_f = resid.astype(jnp.float32)
    row_mean = jnp.mean(resid_f, axis=-1, keepdims=True)
    centred = resid_f - row_mean
    row_var = jnp.mean(centred * centred, axis=-1, keepdims=True)
    return (centred * lax.rsqrt(row_var + NORM_EPS) * gain_vec.astype(jnp.float32)).astype(jnp.bfloat16)


def solution(mesh):
    stages = mesh.shape["pp"]
    next_perm = [(src_stage, (src_stage + 1) % stages) for src_stage in range(stages)]

    def per_device(x_loc, gain_loc, w_in_loc, w_out_loc):
        micro_count, tok_shard = x_loc.shape[0], x_loc.shape[1]
        stage_idx = lax.axis_index("pp")
        rank_idx = lax.axis_index("tp")
        prev_stage = (stage_idx + stages - 1) % stages
        last_work = 2 * micro_count - 1

        def run_tick(tick_idx, loop_state):
            in_box, out_box = loop_state
            work_idx = tick_idx - stage_idx
            active = (work_idx >= 0) & (work_idx <= last_work)
            work_c = jnp.clip(work_idx, 0, last_work)
            virt_idx = work_c // micro_count
            micro_idx = work_c % micro_count
            gain_vec = lax.dynamic_index_in_dim(gain_loc, virt_idx, 0, keepdims=False)[0]
            w_first = lax.dynamic_index_in_dim(w_in_loc, virt_idx, 0, keepdims=False)[0]
            w_second = lax.dynamic_index_in_dim(w_out_loc, virt_idx, 0, keepdims=False)[0]
            cur_shard = lax.dynamic_index_in_dim(in_box, micro_idx, 0, keepdims=False)
            cur_full = lax.all_gather(cur_shard, "tp", axis=0, tiled=True)
            normed = layer_norm(cur_full, gain_vec)
            hidden = jax.nn.gelu(jnp.dot(normed, w_first, preferred_element_type=jnp.float32)).astype(jnp.bfloat16)
            part_prod = jnp.dot(hidden, w_second, preferred_element_type=jnp.float32).astype(jnp.bfloat16)
            reduced = lax.psum(part_prod, "tp")
            own_sum = lax.dynamic_slice_in_dim(reduced, rank_idx * tok_shard, tok_shard, axis=0)
            new_shard = (cur_shard.astype(jnp.float32) + own_sum.astype(jnp.float32)).astype(jnp.bfloat16)
            keep_final = active & (virt_idx == 1) & (stage_idx == stages - 1)
            old_out = lax.dynamic_index_in_dim(out_box, micro_idx, 0, keepdims=False)
            out_box = lax.dynamic_update_index_in_dim(out_box, jnp.where(keep_final, new_shard, old_out), micro_idx, 0)
            received = lax.ppermute(new_shard, "pp", next_perm)
            sent_idx = tick_idx - prev_stage
            store_it = (sent_idx >= 0) & (sent_idx <= last_work) & ((stage_idx != 0) | (sent_idx < micro_count))
            slot_idx = jnp.clip(sent_idx, 0, last_work) % micro_count
            old_in = lax.dynamic_index_in_dim(in_box, slot_idx, 0, keepdims=False)
            in_box = lax.dynamic_update_index_in_dim(in_box, jnp.where(store_it, received, old_in), slot_idx, 0)
            return in_box, out_box

        tick_count = 2 * micro_count + stages - 1
        _, out_box = lax.fori_loop(0, tick_count, run_tick, (x_loc, jnp.zeros_like(x_loc)))
        return lax.psum_scatter(out_box, "pp", scatter_dimension=0, tiled=True)

    return jax.shard_map(per_device, mesh=mesh, in_specs=(P("dp", "tp", None), P(None, "pp", None), P(None, "pp", None, "tp"), P(None, "pp", "tp", None)), out_specs=P(("dp", "pp"), "tp", None), check_vma=False)
```

profile of v0, /device:TPU:121, one launch (start us, length us, event | category | flops | bytes accessed | tf_op | source)
XLA Modules:
  0.0 3263.8 jit_solution(8187830498316676068)
XLA Ops:
  8.6 3226.8 %while.17 = (s32[]{:T(128)}, bf16[16,8,3072]{2,1,0:T(8,128)(2,1)S(1)}, bf16[16,8,3072]{2,1,0:T(8,128)(2,1)S(1)}, s32[]{:T(128)}, pred[]{:T(512)}, /*index=5*/s32...) while((s32[]{:T(128)}, ...), condition=%wide.region_4.5_spmd, body=%wide.region_0.4_spmd.sunk | while | flops 808602752 | bytes 17876924 | solution.py:58
  36.4 58.3 %all-reduce.2.cloned.1.call-done = bf16[64,3072]{1,0:T(8,128)(2,1)} async-done(((bf16[64,3072]{1,0:T(8,128)(2,1)}), bf16[64,3072]{1,0:T(8,128)(2,1)}) %all-reduce.2.cloned.1.call-update) | async-done | bytes 393232 | tf_op jit(solution)/shard_map/while/body/eval_jaxpr/psum | solution.py:43
  98.7 19.8 all-gather.2
  127.5 59.4 %all-reduce.2.cloned.1.call-done = bf16[64,3072]{1,0:T(8,128)(2,1)} async-done(((bf16[64,3072]{1,0:T(8,128)(2,1)}), bf16[64,3072]{1,0:T(8,128)(2,1)}) %all-reduce.2.cloned.1.call-update) | async-done | bytes 393232 | tf_op jit(solution)/shard_map/while/body/eval_jaxpr/psum | solution.py:43
  219.7 59.4 %all-reduce.2.cloned.1.call-done = bf16[64,3072]{1,0:T(8,128)(2,1)} async-done(((bf16[64,3072]{1,0:T(8,128)(2,1)}), bf16[64,3072]{1,0:T(8,128)(2,1)}) %all-reduce.2.cloned.1.call-update) | async-done | bytes 393232 | tf_op jit(solution)/shard_map/while/body/eval_jaxpr/psum | solution.py:43
  283.2 19.8 all-gather.2
  312.0 59.4 %all-reduce.2.cloned.1.call-done = bf16[64,3072]{1,0:T(8,128)(2,1)} async-done(((bf16[64,3072]{1,0:T(8,128)(2,1)}), bf16[64,3072]{1,0:T(8,128)(2,1)}) %all-reduce.2.cloned.1.call-update) | async-done | bytes 393232 | tf_op jit(solution)/shard_map/while/body/eval_jaxpr/psum | solution.py:43
  404.3 59.4 %all-reduce.2.cloned.1.call-done = bf16[64,3072]{1,0:T(8,128)(2,1)} async-done(((bf16[64,3072]{1,0:T(8,128)(2,1)}), bf16[64,3072]{1,0:T(8,128)(2,1)}) %all-reduce.2.cloned.1.call-update) | async-done | bytes 393232 | tf_op jit(solution)/shard_map/while/body/eval_jaxpr/psum | solution.py:43
  496.5 59.4 %all-reduce.2.cloned.1.call-done = bf16[64,3072]{1,0:T(8,128)(2,1)} async-done(((bf16[64,3072]{1,0:T(8,128)(2,1)}), bf16[64,3072]{1,0:T(8,128)(2,1)}) %all-reduce.2.cloned.1.call-update) | async-done | bytes 393232 | tf_op jit(solution)/shard_map/while/body/eval_jaxpr/psum | solution.py:43
  560.0 19.8 all-gather.2
  588.8 59.4 %all-reduce.2.cloned.1.call-done = bf16[64,3072]{1,0:T(8,128)(2,1)} async-done(((bf16[64,3072]{1,0:T(8,128)(2,1)}), bf16[64,3072]{1,0:T(8,128)(2,1)}) %all-reduce.2.cloned.1.call-update) | async-done | bytes 393232 | tf_op jit(solution)/shard_map/while/body/eval_jaxpr/psum | solution.py:43
  681.1 59.4 %all-reduce.2.cloned.1.call-done = bf16[64,3072]{1,0:T(8,128)(2,1)} async-done(((bf16[64,3072]{1,0:T(8,128)(2,1)}), bf16[64,3072]{1,0:T(8,128)(2,1)}) %all-reduce.2.cloned.1.call-update) | async-done | bytes 393232 | tf_op jit(solution)/shard_map/while/body/eval_jaxpr/psum | solution.py:43
  773.3 59.4 %all-reduce.2.cloned.1.call-done = bf16[64,3072]{1,0:T(8,128)(2,1)} async-done(((bf16[64,3072]{1,0:T(8,128)(2,1)}), bf16[64,3072]{1,0:T(8,128)(2,1)}) %all-reduce.2.cloned.1.call-update) | async-done | bytes 393232 | tf_op jit(solution)/shard_map/while/body/eval_jaxpr/psum | solution.py:43
  836.8 19.8 all-gather.2
  865.6 59.4 %all-reduce.2.cloned.1.call-done = bf16[64,3072]{1,0:T(8,128)(2,1)} async-done(((bf16[64,3072]{1,0:T(8,128)(2,1)}), bf16[64,3072]{1,0:T(8,128)(2,1)}) %all-reduce.2.cloned.1.call-update) | async-done | bytes 393232 | tf_op jit(solution)/shard_map/while/body/eval_jaxpr/psum | solution.py:43
  957.8 59.4 %all-reduce.2.cloned.1.call-done = bf16[64,3072]{1,0:T(8,128)(2,1)} async-done(((bf16[64,3072]{1,0:T(8,128)(2,1)}), bf16[64,3072]{1,0:T(8,128)(2,1)}) %all-reduce.2.cloned.1.call-update) | async-done | bytes 393232 | tf_op jit(solution)/shard_map/while/body/eval_jaxpr/psum | solution.py:43
  1050.1 59.4 %all-reduce.2.cloned.1.call-done = bf16[64,3072]{1,0:T(8,128)(2,1)} async-done(((bf16[64,3072]{1,0:T(8,128)(2,1)}), bf16[64,3072]{1,0:T(8,128)(2,1)}) %all-reduce.2.cloned.1.call-update) | async-done | bytes 393232 | tf_op jit(solution)/shard_map/while/body/eval_jaxpr/psum | solution.py:43
  1142.4 59.4 %all-reduce.2.cloned.1.call-done = bf16[64,3072]{1,0:T(8,128)(2,1)} async-done(((bf16[64,3072]{1,0:T(8,128)(2,1)}), bf16[64,3072]{1,0:T(8,128)(2,1)}) %all-reduce.2.cloned.1.call-update) | async-done | bytes 393232 | tf_op jit(solution)/shard_map/while/body/eval_jaxpr/psum | solution.py:43
  1234.6 59.4 %all-reduce.2.cloned.1.call-done = bf16[64,3072]{1,0:T(8,128)(2,1)} async-done(((bf16[64,3072]{1,0:T(8,128)(2,1)}), bf16[64,3072]{1,0:T(8,128)(2,1)}) %all-reduce.2.cloned.1.call-update) | async-done | bytes 393232 | tf_op jit(solution)/shard_map/while/body/eval_jaxpr/psum | solution.py:43
  1298.1 19.8 all-gather.2
  1326.9 59.4 %all-reduce.2.cloned.1.call-done = bf16[64,3072]{1,0:T(8,128)(2,1)} async-done(((bf16[64,3072]{1,0:T(8,128)(2,1)}), bf16[64,3072]{1,0:T(8,128)(2,1)}) %all-reduce.2.cloned.1.call-update) | async-done | bytes 393232 | tf_op jit(solution)/shard_map/while/body/eval_jaxpr/psum | solution.py:43
  1419.1 59.4 %all-reduce.2.cloned.1.call-done = bf16[64,3072]{1,0:T(8,128)(2,1)} async-done(((bf16[64,3072]{1,0:T(8,128)(2,1)}), bf16[64,3072]{1,0:T(8,128)(2,1)}) %all-reduce.2.cloned.1.call-update) | async-done | bytes 393232 | tf_op jit(solution)/shard_map/while/body/eval_jaxpr/psum | solution.py:43
  1511.4 59.4 %all-reduce.2.cloned.1.call-done = bf16[64,3072]{1,0:T(8,128)(2,1)} async-done(((bf16[64,3072]{1,0:T(8,128)(2,1)}), bf16[64,3072]{1,0:T(8,128)(2,1)}) %all-reduce.2.cloned.1.call-update) | async-done | bytes 393232 | tf_op jit(solution)/shard_map/while/body/eval_jaxpr/psum | solution.py:43
  1574.8 19.8 all-gather.2
  1603.7 59.4 %all-reduce.2.cloned.1.call-done = bf16[64,3072]{1,0:T(8,128)(2,1)} async-done(((bf16[64,3072]{1,0:T(8,128)(2,1)}), bf16[64,3072]{1,0:T(8,128)(2,1)}) %all-reduce.2.cloned.1.call-update) | async-done | bytes 393232 | tf_op jit(solution)/shard_map/while/body/eval_jaxpr/psum | solution.py:43
  1695.9 59.4 %all-reduce.2.cloned.1.call-done = bf16[64,3072]{1,0:T(8,128)(2,1)} async-done(((bf16[64,3072]{1,0:T(8,128)(2,1)}), bf16[64,3072]{1,0:T(8,128)(2,1)}) %all-reduce.2.cloned.1.call-update) | async-done | bytes 393232 | tf_op jit(solution)/shard_map/while/body/eval_jaxpr/psum | solution.py:43
  1788.2 59.4 %all-reduce.2.cloned.1.call-done = bf16[64,3072]{1,0:T(8,128)(2,1)} async-done(((bf16[64,3072]{1,0:T(8,128)(2,1)}), bf16[64,3072]{1,0:T(8,128)(2,1)}) %all-reduce.2.cloned.1.call-update) | async-done | bytes 393232 | tf_op jit(solution)/shard_map/while/body/eval_jaxpr/psum | solution.py:43
  1851.6 19.8 all-gather.2
  1880.4 59.4 %all-reduce.2.cloned.1.call-done = bf16[64,3072]{1,0:T(8,128)(2,1)} async-done(((bf16[64,3072]{1,0:T(8,128)(2,1)}), bf16[64,3072]{1,0:T(8,128)(2,1)}) %all-reduce.2.cloned.1.call-update) | async-done | bytes 393232 | tf_op jit(solution)/shard_map/while/body/eval_jaxpr/psum | solution.py:43
  1972.7 59.4 %all-reduce.2.cloned.1.call-done = bf16[64,3072]{1,0:T(8,128)(2,1)} async-done(((bf16[64,3072]{1,0:T(8,128)(2,1)}), bf16[64,3072]{1,0:T(8,128)(2,1)}) %all-reduce.2.cloned.1.call-update) | async-done | bytes 393232 | tf_op jit(solution)/shard_map/while/body/eval_jaxpr/psum | solution.py:43
  2036.2 19.8 all-gather.2
  2065.0 59.4 %all-reduce.2.cloned.1.call-done = bf16[64,3072]{1,0:T(8,128)(2,1)} async-done(((bf16[64,3072]{1,0:T(8,128)(2,1)}), bf16[64,3072]{1,0:T(8,128)(2,1)}) %all-reduce.2.cloned.1.call-update) | async-done | bytes 393232 | tf_op jit(solution)/shard_map/while/body/eval_jaxpr/psum | solution.py:43
  2157.2 59.4 %all-reduce.2.cloned.1.call-done = bf16[64,3072]{1,0:T(8,128)(2,1)} async-done(((bf16[64,3072]{1,0:T(8,128)(2,1)}), bf16[64,3072]{1,0:T(8,128)(2,1)}) %all-reduce.2.cloned.1.call-update) | async-done | bytes 393232 | tf_op jit(solution)/shard_map/while/body/eval_jaxpr/psum | solution.py:43
  2249.5 59.4 %all-reduce.2.cloned.1.call-done = bf16[64,3072]{1,0:T(8,128)(2,1)} async-done(((bf16[64,3072]{1,0:T(8,128)(2,1)}), bf16[64,3072]{1,0:T(8,128)(2,1)}) %all-reduce.2.cloned.1.call-update) | async-done | bytes 393232 | tf_op jit(solution)/shard_map/while/body/eval_jaxpr/psum | solution.py:43
  2312.9 19.8 all-gather.2
  2341.8 59.4 %all-reduce.2.cloned.1.call-done = bf16[64,3072]{1,0:T(8,128)(2,1)} async-done(((bf16[64,3072]{1,0:T(8,128)(2,1)}), bf16[64,3072]{1,0:T(8,128)(2,1)}) %all-reduce.2.cloned.1.call-update) | async-done | bytes 393232 | tf_op jit(solution)/shard_map/while/body/eval_jaxpr/psum | solution.py:43
  2434.0 59.4 %all-reduce.2.cloned.1.call-done = bf16[64,3072]{1,0:T(8,128)(2,1)} async-done(((bf16[64,3072]{1,0:T(8,128)(2,1)}), bf16[64,3072]{1,0:T(8,128)(2,1)}) %all-reduce.2.cloned.1.call-update) | async-done | bytes 393232 | tf_op jit(solution)/shard_map/while/body/eval_jaxpr/psum | solution.py:43
  2526.3 59.4 %all-reduce.2.cloned.1.call-done = bf16[64,3072]{1,0:T(8,128)(2,1)} async-done(((bf16[64,3072]{1,0:T(8,128)(2,1)}), bf16[64,3072]{1,0:T(8,128)(2,1)}) %all-reduce.2.cloned.1.call-update) | async-done | bytes 393232 | tf_op jit(solution)/shard_map/while/body/eval_jaxpr/psum | solution.py:43
  2589.7 19.8 all-gather.2
  2618.5 59.4 %all-reduce.2.cloned.1.call-done = bf16[64,3072]{1,0:T(8,128)(2,1)} async-done(((bf16[64,3072]{1,0:T(8,128)(2,1)}), bf16[64,3072]{1,0:T(8,128)(2,1)}) %all-reduce.2.cloned.1.call-update) | async-done | bytes 393232 | tf_op jit(solution)/shard_map/while/body/eval_jaxpr/psum | solution.py:43
  2710.8 59.4 %all-reduce.2.cloned.1.call-done = bf16[64,3072]{1,0:T(8,128)(2,1)} async-done(((bf16[64,3072]{1,0:T(8,128)(2,1)}), bf16[64,3072]{1,0:T(8,128)(2,1)}) %all-reduce.2.cloned.1.call-update) | async-done | bytes 393232 | tf_op jit(solution)/shard_map/while/body/eval_jaxpr/psum | solution.py:43
  2803.1 59.4 %all-reduce.2.cloned.1.call-done = bf16[64,3072]{1,0:T(8,128)(2,1)} async-done(((bf16[64,3072]{1,0:T(8,128)(2,1)}), bf16[64,3072]{1,0:T(8,128)(2,1)}) %all-reduce.2.cloned.1.call-update) | async-done | bytes 393232 | tf_op jit(solution)/shard_map/while/body/eval_jaxpr/psum | solution.py:43
  2895.3 59.4 %all-reduce.2.cloned.1.call-done = bf16[64,3072]{1,0:T(8,128)(2,1)} async-done(((bf16[64,3072]{1,0:T(8,128)(2,1)}), bf16[64,3072]{1,0:T(8,128)(2,1)}) %all-reduce.2.cloned.1.call-update) | async-done | bytes 393232 | tf_op jit(solution)/shard_map/while/body/eval_jaxpr/psum | solution.py:43
  2987.6 59.4 %all-reduce.2.cloned.1.call-done = bf16[64,3072]{1,0:T(8,128)(2,1)} async-done(((bf16[64,3072]{1,0:T(8,128)(2,1)}), bf16[64,3072]{1,0:T(8,128)(2,1)}) %all-reduce.2.cloned.1.call-update) | async-done | bytes 393232 | tf_op jit(solution)/shard_map/while/body/eval_jaxpr/psum | solution.py:43
  3051.0 19.8 all-gather.2
  3079.8 59.4 %all-reduce.2.cloned.1.call-done = bf16[64,3072]{1,0:T(8,128)(2,1)} async-done(((bf16[64,3072]{1,0:T(8,128)(2,1)}), bf16[64,3072]{1,0:T(8,128)(2,1)}) %all-reduce.2.cloned.1.call-update) | async-done | bytes 393232 | tf_op jit(solution)/shard_map/while/body/eval_jaxpr/psum | solution.py:43
  3172.1 59.4 %all-reduce.2.cloned.1.call-done = bf16[64,3072]{1,0:T(8,128)(2,1)} async-done(((bf16[64,3072]{1,0:T(8,128)(2,1)}), bf16[64,3072]{1,0:T(8,128)(2,1)}) %all-reduce.2.cloned.1.call-update) | async-done | bytes 393232 | tf_op jit(solution)/shard_map/while/body/eval_jaxpr/psum | solution.py:43
  3236.4 20.3 reduce-scatter.2.cloned.1.call-done
  (520 shorter events, 928.5 us)
Async XLA Ops:
  8.6 86.0 %all-reduce.2.cloned.1.call-start = ((), (), s32[]{:S(2)}) async-start(), calls=%async_computation.2 | async-start | bytes 786432 | tf_op jit(solution)/shard_map/while/body/eval_jaxpr/psum | solution.py:43
  98.5 88.4 %all-reduce.2.cloned.1.call-start = ((), (), s32[]{:S(2)}) async-start(), calls=%async_computation.2 | async-start | bytes 786432 | tf_op jit(solution)/shard_map/while/body/eval_jaxpr/psum | solution.py:43
  190.8 88.4 %all-reduce.2.cloned.1.call-start = ((), (), s32[]{:S(2)}) async-start(), calls=%async_computation.2 | async-start | bytes 786432 | tf_op jit(solution)/shard_map/while/body/eval_jaxpr/psum | solution.py:43
  280.0 3.0 collective-permute-start
  283.1 88.4 %all-reduce.2.cloned.1.call-start = ((), (), s32[]{:S(2)}) async-start(), calls=%async_computation.2 | async-start | bytes 786432 | tf_op jit(solution)/shard_map/while/body/eval_jaxpr/psum | solution.py:43
  375.3 88.4 %all-reduce.2.cloned.1.call-start = ((), (), s32[]{:S(2)}) async-start(), calls=%async_computation.2 | async-start | bytes 786432 | tf_op jit(solution)/shard_map/while/body/eval_jaxpr/psum | solution.py:43
  467.6 88.4 %all-reduce.2.cloned.1.call-start = ((), (), s32[]{:S(2)}) async-start(), calls=%async_computation.2 | async-start | bytes 786432 | tf_op jit(solution)/shard_map/while/body/eval_jaxpr/psum | solution.py:43
  556.8 3.0 collective-permute-start
  559.8 88.4 %all-reduce.2.cloned.1.call-start = ((), (), s32[]{:S(2)}) async-start(), calls=%async_computation.2 | async-start | bytes 786432 | tf_op jit(solution)/shard_map/while/body/eval_jaxpr/psum | solution.py:43
  652.1 88.4 %all-reduce.2.cloned.1.call-start = ((), (), s32[]{:S(2)}) async-start(), calls=%async_computation.2 | async-start | bytes 786432 | tf_op jit(solution)/shard_map/while/body/eval_jaxpr/psum | solution.py:43
  744.4 88.4 %all-reduce.2.cloned.1.call-start = ((), (), s32[]{:S(2)}) async-start(), calls=%async_computation.2 | async-start | bytes 786432 | tf_op jit(solution)/shard_map/while/body/eval_jaxpr/psum | solution.py:43
  833.6 3.0 collective-permute-start
  836.6 88.4 %all-reduce.2.cloned.1.call-start = ((), (), s32[]{:S(2)}) async-start(), calls=%async_computation.2 | async-start | bytes 786432 | tf_op jit(solution)/shard_map/while/body/eval_jaxpr/psum | solution.py:43
  928.9 88.4 %all-reduce.2.cloned.1.call-start = ((), (), s32[]{:S(2)}) async-start(), calls=%async_computation.2 | async-start | bytes 786432 | tf_op jit(solution)/shard_map/while/body/eval_jaxpr/psum | solution.py:43
  1021.2 88.4 %all-reduce.2.cloned.1.call-start = ((), (), s32[]{:S(2)}) async-start(), calls=%async_computation.2 | async-start | bytes 786432 | tf_op jit(solution)/shard_map/while/body/eval_jaxpr/psum | solution.py:43
  1110.4 3.0 collective-permute-start
  1113.4 88.4 %all-reduce.2.cloned.1.call-start = ((), (), s32[]{:S(2)}) async-start(), calls=%async_computation.2 | async-start | bytes 786432 | tf_op jit(solution)/shard_map/while/body/eval_jaxpr/psum | solution.py:43
  1205.7 88.4 %all-reduce.2.cloned.1.call-start = ((), (), s32[]{:S(2)}) async-start(), calls=%async_computation.2 | async-start | bytes 786432 | tf_op jit(solution)/shard_map/while/body/eval_jaxpr/psum | solution.py:43
  1294.9 3.0 collective-permute-start
  1297.9 88.4 %all-reduce.2.cloned.1.call-start = ((), (), s32[]{:S(2)}) async-start(), calls=%async_computation.2 | async-start | bytes 786432 | tf_op jit(solution)/shard_map/while/body/eval_jaxpr/psum | solution.py:43
  1390.2 88.4 %all-reduce.2.cloned.1.call-start = ((), (), s32[]{:S(2)}) async-start(), calls=%async_computation.2 | async-start | bytes 786432 | tf_op jit(solution)/shard_map/while/body/eval_jaxpr/psum | solution.py:43
  1482.5 88.4 %all-reduce.2.cloned.1.call-start = ((), (), s32[]{:S(2)}) async-start(), calls=%async_computation.2 | async-start | bytes 786432 | tf_op jit(solution)/shard_map/while/body/eval_jaxpr/psum | solution.py:43
  1571.7 3.0 collective-permute-start
  1574.7 88.4 %all-reduce.2.cloned.1.call-start = ((), (), s32[]{:S(2)}) async-start(), calls=%async_computation.2 | async-start | bytes 786432 | tf_op jit(solution)/shard_map/while/body/eval_jaxpr/psum | solution.py:43
  1667.0 88.4 %all-reduce.2.cloned.1.call-start = ((), (), s32[]{:S(2)}) async-start(), calls=%async_computation.2 | async-start | bytes 786432 | tf_op jit(solution)/shard_map/while/body/eval_jaxpr/psum | solution.py:43
  1759.2 88.4 %all-reduce.2.cloned.1.call-start = ((), (), s32[]{:S(2)}) async-start(), calls=%async_computation.2 | async-start | bytes 786432 | tf_op jit(solution)/shard_map/while/body/eval_jaxpr/psum | solution.py:43
  1848.4 3.0 collective-permute-start
  1851.5 88.4 %all-reduce.2.cloned.1.call-start = ((), (), s32[]{:S(2)}) async-start(), calls=%async_computation.2 | async-start | bytes 786432 | tf_op jit(solution)/shard_map/while/body/eval_jaxpr/psum | solution.py:43
  1943.8 88.4 %all-reduce.2.cloned.1.call-start = ((), (), s32[]{:S(2)}) async-start(), calls=%async_computation.2 | async-start | bytes 786432 | tf_op jit(solution)/shard_map/while/body/eval_jaxpr/psum | solution.py:43
  2033.0 3.0 collective-permute-start
  2036.0 88.4 %all-reduce.2.cloned.1.call-start = ((), (), s32[]{:S(2)}) async-start(), calls=%async_computation.2 | async-start | bytes 786432 | tf_op jit(solution)/shard_map/while/body/eval_jaxpr/psum | solution.py:43
  2128.3 88.4 %all-reduce.2.cloned.1.call-start = ((), (), s32[]{:S(2)}) async-start(), calls=%async_computation.2 | async-start | bytes 786432 | tf_op jit(solution)/shard_map/while/body/eval_jaxpr/psum | solution.py:43
  2220.5 88.4 %all-reduce.2.cloned.1.call-start = ((), (), s32[]{:S(2)}) async-start(), calls=%async_computation.2 | async-start | bytes 786432 | tf_op jit(solution)/shard_map/while/body/eval_jaxpr/psum | solution.py:43
  2309.7 3.0 collective-permute-start
  2312.8 88.4 %all-reduce.2.cloned.1.call-start = ((), (), s32[]{:S(2)}) async-start(), calls=%async_computation.2 | async-start | bytes 786432 | tf_op jit(solution)/shard_map/while/body/eval_jaxpr/psum | solution.py:43
  2405.1 88.4 %all-reduce.2.cloned.1.call-start = ((), (), s32[]{:S(2)}) async-start(), calls=%async_computation.2 | async-start | bytes 786432 | tf_op jit(solution)/shard_map/while/body/eval_jaxpr/psum | solution.py:43
  2497.3 88.4 %all-reduce.2.cloned.1.call-start = ((), (), s32[]{:S(2)}) async-start(), calls=%async_computation.2 | async-start | bytes 786432 | tf_op jit(solution)/shard_map/while/body/eval_jaxpr/psum | solution.py:43
  2586.5 3.0 collective-permute-start
  2589.6 88.4 %all-reduce.2.cloned.1.call-start = ((), (), s32[]{:S(2)}) async-start(), calls=%async_computation.2 | async-start | bytes 786432 | tf_op jit(solution)/shard_map/while/body/eval_jaxpr/psum | solution.py:43
  2681.9 88.4 %all-reduce.2.cloned.1.call-start = ((), (), s32[]{:S(2)}) async-start(), calls=%async_computation.2 | async-start | bytes 786432 | tf_op jit(solution)/shard_map/while/body/eval_jaxpr/psum | solution.py:43
  2774.1 88.4 %all-reduce.2.cloned.1.call-start = ((), (), s32[]{:S(2)}) async-start(), calls=%async_computation.2 | async-start | bytes 786432 | tf_op jit(solution)/shard_map/while/body/eval_jaxpr/psum | solution.py:43
  2863.3 3.0 collective-permute-start
  2866.4 88.4 %all-reduce.2.cloned.1.call-start = ((), (), s32[]{:S(2)}) async-start(), calls=%async_computation.2 | async-start | bytes 786432 | tf_op jit(solution)/shard_map/while/body/eval_jaxpr/psum | solution.py:43
  2958.6 88.4 %all-reduce.2.cloned.1.call-start = ((), (), s32[]{:S(2)}) async-start(), calls=%async_computation.2 | async-start | bytes 786432 | tf_op jit(solution)/shard_map/while/body/eval_jaxpr/psum | solution.py:43
  3047.8 3.0 collective-permute-start
  3050.9 88.4 %all-reduce.2.cloned.1.call-start = ((), (), s32[]{:S(2)}) async-start(), calls=%async_computation.2 | async-start | bytes 786432 | tf_op jit(solution)/shard_map/while/body/eval_jaxpr/psum | solution.py:43
  3143.2 88.4 %all-reduce.2.cloned.1.call-start = ((), (), s32[]{:S(2)}) async-start(), calls=%async_computation.2 | async-start | bytes 786432 | tf_op jit(solution)/shard_map/while/body/eval_jaxpr/psum | solution.py:43
  3235.4 21.2 reduce-scatter.2.cloned.1.call-start
  (24 other events, 70.5 us)
Sparse Core Ops, SparseCore 0:
  36.4 58.1 all-reduce.1
  127.6 59.2 all-reduce.1
  219.8 59.2 all-reduce.1
  312.1 59.2 all-reduce.1
  404.4 59.2 all-reduce.1
  496.6 59.2 all-reduce.1
  588.9 59.2 all-reduce.1
  681.1 59.2 all-reduce.1
  773.4 59.2 all-reduce.1
  865.7 59.2 all-reduce.1
  957.9 59.2 all-reduce.1
  1050.2 59.2 all-reduce.1
  1142.4 59.2 all-reduce.1
  1234.7 59.2 all-reduce.1
  1327.0 59.2 all-reduce.1
  1419.2 59.2 all-reduce.1
  1511.5 59.2 all-reduce.1
  1603.7 59.2 all-reduce.1
  1696.0 59.2 all-reduce.1
  1788.3 59.2 all-reduce.1
  1880.5 59.2 all-reduce.1
  1972.8 59.2 all-reduce.1
  2065.1 59.2 all-reduce.1
  2157.3 59.2 all-reduce.1
  2249.6 59.2 all-reduce.1
  2341.8 59.2 all-reduce.1
  2434.1 59.2 all-reduce.1
  2526.4 59.2 all-reduce.1
  2618.6 59.2 all-reduce.1
  2710.9 59.2 all-reduce.1
  2803.1 59.2 all-reduce.1
  2895.4 59.2 all-reduce.1
  2987.7 59.2 all-reduce.1
  3079.9 59.2 all-reduce.1
  3172.2 59.2 all-reduce.1
Sparse Core Ops, SparseCore 1:
  3238.2 18.3 reduce-scatter.1
where the time goes:
time: 3270 us; the launch traced here: 3260 us
  waiting for transfers between devices  2200 us (67%)
  blocking collectives  691 us (21%)
  matrix products  272 us (8%)
  other arithmetic  70.3 us (2%)
    psum x35, waiting for transfers between devices, run_tick(): reduced = lax.psum(part_prod, 'tp')  2080 us
    all_gather x35, blocking collectives, run_tick(): cur_full = lax.all_gather(cur_shard, 'tp', axis=0, tiled=True)  691 us
    dot_general x35, matrix products, run_tick(): jnp.dot(hidden, w_second, preferred_element_type=jnp.float32)  272 us
    ppermute x35, waiting for transfers between devices, run_tick(): received = lax.ppermute(new_shard, 'pp', next_perm)  96.3 us
  transfers between devices with their start and end apart: 71, of which 71 were waited for; matrix products, arithmetic and copies ran while one was open for 0% of the time, Pallas kernels for 0%

commit v1 on v0

v1 whole, which is shorter than its diff:
```python
import functools

import jax
import jax.numpy as jnp
from jax import lax
from jax.experimental import pallas as pl
from jax.experimental.pallas import tpu as pltpu
from jax.sharding import PartitionSpec as P

MESH = pl.DeviceIdType.MESH
NORM_EPS = 1e-5
CORES = 2
LOOKAHEAD = 2


def _f32(a):
    return a.astype(jnp.float32)


def _bf16(a):
    return a.astype(jnp.bfloat16)


def _kernel(dims, x_hbm, gain_ref, w1_hbm, w2_hbm, out_ref,
            w1, w2, xs, xbuf, ybuf, rbuf, hbuf, abuf, sbuf, fbuf, obuf,
            wl_sem, wp_send, wp_recv, xl_sem, x_send, x_recv,
            rs_send, rs_recv, ag_send, ag_recv, f_send, f_recv):
    stages, chips, visits, tok, width, hid = dims
    ranks = chips * CORES
    slab = width // chips
    tsh = tok // ranks
    p = lax.axis_index("pp")
    t = lax.axis_index("tp")
    c = t // CORES
    k = lax.rem(t, CORES)
    nxt = lax.rem(p + 1, stages)
    at_start = p == 0
    at_end = p == stages - 1

    def dev(pp, chip, core):
        return {"pp": pp, "tp": chip * CORES + core}

    def remote(src, dst, ssem, rsem, where):
        return pltpu.make_async_remote_copy(src_ref=src, dst_ref=dst, send_sem=ssem, recv_sem=rsem,
                                            device_id=where, device_id_type=MESH)

    def local_wait(ref, sem):
        pltpu.make_async_copy(ref, ref, sem).wait()

    def load_w(v):
        return (pltpu.make_async_copy(w1_hbm.at[v], w1.at[v, k], wl_sem.at[v, 0]),
                pltpu.make_async_copy(w2_hbm.at[v], w2.at[v, k], wl_sem.at[v, 1]))

    def push_w(v):
        other = dev(p, c, 1 - k)
        return (remote(w1_hbm.at[v], w1.at[v, k], wp_send.at[v, 0], wp_recv.at[v, 0], other),
                remote(w2_hbm.at[v], w2.at[v, k], wp_send.at[v, 1], wp_recv.at[v, 1], other))

    x_load = pltpu.make_async_copy(x_hbm, xs, xl_sem)
    x_load.start()
    for v in range(2):
        for cp in load_w(v):
            cp.start()

    bar = pltpu.get_barrier_semaphore()
    for pp in range(stages):
        for tt in range(ranks):
            @pl.when((pp != p) | (tt != t))
            def _(pp=pp, tt=tt):
                pl.semaphore_signal(bar, inc=1, device_id={"pp": pp, "tp": tt}, device_id_type=MESH)
    pl.semaphore_wait(bar, stages * ranks - 1)
    x_load.wait()

    def x_copy(i, core, chip):
        return remote(xs.at[CORES * i + core], xbuf.at[i, t], x_send.at[chip], x_recv.at[i, t], dev(p, chip, core))

    def x_share(i):
        xbuf[i, t] = xs[CORES * i + k]
        for d in range(1, chips):
            for dk in range(CORES):
                x_copy(i, lax.rem(k + dk, CORES), lax.rem(c + d, chips)).start()

    @pl.when(at_start)
    def _():
        for i in range(visits):
            x_copy(i, 1 - k, c).start()
        for i in range(LOOKAHEAD):
            x_share(i)

    for v in range(2):
        for cp in push_w(v):
            cp.start()

    def visit(idx, carry):
        v = idx // visits
        i = lax.rem(idx, visits)
        par = lax.rem(idx, 2)
        first = at_start & (v == 0)
        last = at_end & (v == 1)

        @pl.when(first & (i + LOOKAHEAD < visits))
        def _():
            x_share(i + LOOKAHEAD)

        @pl.when(first)
        def _():
            for r in range(ranks):
                @pl.when(r != t)
                def _(r=r):
                    local_wait(xbuf.at[i, r], x_recv.at[i, r])
            for q in range(chips):
                ybuf[i, q] = _bf16(_f32(xbuf[i, :, :, q * slab:(q + 1) * slab]).reshape(tok, slab))

        def ag_copy(d):
            return remote(ybuf.at[i, c], ybuf.at[i, c], ag_send.at[par, d - 1], ag_recv.at[i, c],
                          dev(p, lax.rem(c + d, chips), k))

        @pl.when(jnp.logical_not(first))
        def _():
            for q in range(chips):
                local_wait(rbuf.at[i, q], rs_recv.at[i, q])
            total = _f32(rbuf[i, 0])
            for q in range(1, chips):
                total = total + _f32(rbuf[i, q])
            ybuf[i, c] = _bf16(total)
            for d in (2, 1, 3):
                ag_copy(d).start()
            for d in range(1, chips):
                q = lax.rem(c + d, chips)
                local_wait(ybuf.at[i, q], ag_recv.at[i, q])
            for d in range(1, chips):
                ag_copy(d).wait_send()

        part = [_f32(ybuf[i, q]) for q in range(chips)]
        mean = sum(jnp.sum(a, axis=-1, keepdims=True) for a in part) * (1.0 / width)
        var = jnp.zeros_like(mean)
        for q in range(chips):
            a = _f32(ybuf[i, q]) - mean
            var = var + jnp.sum(a * a, axis=-1, keepdims=True)
        scale = lax.rsqrt(var * (1.0 / width) + NORM_EPS)
        for q in range(chips):
            cols = slice(q * slab, (q + 1) * slab)
            hbuf[:, cols] = _bf16((_f32(ybuf[i, q]) - mean) * scale * _f32(gain_ref[v, :, cols]))

        def wait_weights(j):
            @pl.when(i == 0)
            def _():
                load_w(v)[j].wait()
                push_w(v)[j].wait_recv()

        wait_weights(0)
        for s in range(CORES):
            for n in range(0, hid, 512):
                acc = jnp.dot(hbuf[...], w1[v, s, :, n:n + 512], preferred_element_type=jnp.float32)
                abuf[s, :, n:n + 512] = _bf16(jax.nn.gelu(acc))
        wait_weights(1)

        def rs_copy(d):
            return remote(sbuf.at[par, d], rbuf.at[i, c], rs_send.at[par, d], rs_recv.at[i, c],
                          dev(nxt, lax.rem(c + d, chips), k))

        for d in (2, 1, 3, 0):
            q = lax.rem(c + d, chips)
            cols = pl.ds(pl.multiple_of(q * slab, slab), slab)
            prod = jnp.zeros((tok, slab), jnp.float32)
            for s in range(CORES):
                prod = prod + _f32(_bf16(jnp.dot(abuf[s], w2[v, s, :, cols], preferred_element_type=jnp.float32)))

            @pl.when(jnp.logical_not(last))
            def _():
                @pl.when(idx >= 2)
                def _():
                    rs_copy(d).wait_send()
                if d == 0:
                    sbuf[par, d] = _bf16(prod + _f32(ybuf[i, c]))
                else:
                    sbuf[par, d] = _bf16(prod)
                rs_copy(d).start()

            @pl.when(last)
            def _():
                row_chip = lax.broadcasted_iota(jnp.int32, (tok, slab), 0) // (tsh * CORES)
                resid = jnp.where(row_chip == c, _f32(ybuf[i, q]), 0.0)
                fbuf[:, :, cols] = _bf16((prod + resid).reshape(ranks, tsh, slab))

        @pl.when(last)
        def _():
            dst_stage = (CORES * i) // (visits * CORES // stages)
            slot = lax.rem(CORES * i, visits * CORES // stages) + k

            def f_copy(r):
                return remote(fbuf.at[r], obuf.at[slot, c], f_send.at[r], f_recv.at[slot, c], {"pp": dst_stage, "tp": r})

            for r in range(ranks):
                mine = (dst_stage == p) & (r == t)

                @pl.when(mine)
                def _(r=r):
                    obuf[slot, c] = fbuf[r]

                @pl.when(jnp.logical_not(mine))
                def _(r=r):
                    f_copy(r).start()
            for r in range(ranks):
                @pl.when((dst_stage != p) | (r != t))
                def _(r=r):
                    f_copy(r).wait_send()
        return carry

    lax.fori_loop(0, 2 * visits, visit, 0)

    per_stage = visits * CORES // stages
    for j in range(per_stage):
        for q in range(chips):
            mine = at_end & (q == c) & (k == j % CORES)

            @pl.when(jnp.logical_not(mine))
            def _(j=j, q=q):
                local_wait(obuf.at[j, q], f_recv.at[j, q])
        total = _f32(obuf[j, 0])
        for q in range(1, chips):
            total = total + _f32(obuf[j, q])
        out_ref[j] = _bf16(total)

    for par in range(2):
        for d in range(chips):
            local_wait(sbuf.at[par, d], rs_send.at[par, d])
    for v in range(2):
        for cp in push_w(v):
            cp.wait_send()

    @pl.when(at_start)
    def _():
        for d in range(chips):
            chip = lax.rem(c + d, chips)
            ref = xs.at[pl.ds(0, visits)] if d == 0 else xs
            local_wait(ref, x_send.at[chip])


def solution(mesh):
    stages, ranks = mesh.shape["pp"], mesh.shape["tp"]
    chips = ranks // CORES

    def per_device(x, gain, w_in, w_out):
        micro, tsh, width = x.shape
        passes, _, _, hid = w_in.shape
        tok = tsh * ranks
        visits = micro // CORES
        slab = width // chips
        per_stage = micro // stages
        dims = (stages, chips, visits, tok, width, hid)
        bf = jnp.bfloat16
        dma = pltpu.SemaphoreType.DMA
        any_space = pl.BlockSpec(memory_space=pl.ANY)
        vmem = pl.BlockSpec(memory_space=pltpu.VMEM)
        return pl.pallas_call(
            functools.partial(_kernel, dims),
            name="mlp_pipe",
            out_shape=jax.ShapeDtypeStruct((per_stage, tsh, width), bf),
            in_specs=[any_space, vmem, any_space, any_space],
            out_specs=vmem,
            scratch_shapes=[
                pltpu.VMEM((passes, CORES, width, hid), bf),
                pltpu.VMEM((passes, CORES, hid, width), bf),
                pltpu.VMEM((micro, tsh, width), bf),
                pltpu.VMEM((visits, ranks, tsh, width), bf),
                pltpu.VMEM((visits, chips, tok, slab), bf),
                pltpu.VMEM((visits, chips, tok, slab), bf),
                pltpu.VMEM((tok, width), bf),
                pltpu.VMEM((CORES, tok, hid), bf),
                pltpu.VMEM((2, chips, tok, slab), bf),
                pltpu.VMEM((ranks, tsh, width), bf),
                pltpu.VMEM((per_stage, chips, tsh, width), bf),
                dma((passes, 2)), dma((passes, 2)), dma((passes, 2)),
                dma, dma((chips,)), dma((visits, ranks)),
                dma((2, chips)), dma((visits, chips)), dma((2, chips - 1)), dma((visits, chips)),
                dma((ranks,)), dma((per_stage, chips)),
            ],
            compiler_params=pltpu.CompilerParams(collective_id=0, has_side_effects=True, vmem_limit_bytes=67043328),
        )(x, gain, w_in.reshape(passes, width, hid), w_out.reshape(passes, hid, width))

    return jax.shard_map(
        per_device,
        mesh=mesh,
        in_specs=(P("dp", "tp", None), P(None, "pp", None), P(None, "pp", None, "tp"), P(None, "pp", "tp", None)),
        out_specs=P(("dp", "pp"), "tp", None),
        check_vma=False,
    )
```

time: 3270 us -> 351 us (0.11)
  waiting for transfers between devices: 2200 us -> 0 us
  blocking collectives: 691 us -> 0 us
  Pallas kernels: 0 us -> 348 us
  matrix products: 272 us -> 0 us
  other arithmetic: 70.3 us -> 0 us
    psum x35 -> x0, waiting for transfers between devices: 2080 us -> none  [run_tick(): reduced = lax.psum(part_prod, 'tp')]
    all_gather x35 -> x0, blocking collectives: 691 us -> none  [run_tick(): cur_full = lax.all_gather(cur_shard, 'tp', axis=0, tiled=True)]
    pallas_call x0 -> x1, Pallas kernels: none -> 348 us  [per_device(): pl.pallas_call(functools.partial(_kernel, dims), name='mlp_pipe', out_sha...]
    dot_general x35 -> x0, matrix products: 272 us -> none  [run_tick(): jnp.dot(hidden, w_second, preferred_element_type=jnp.float32)]
    ppermute x35 -> x0, waiting for transfers between devices: 96.3 us -> none  [run_tick(): received = lax.ppermute(new_shard, 'pp', next_perm)]
  transfers between devices with their start and end apart: 71 -> 0, of which waited for: 71 -> 0; matrix products, arithmetic and copies ran while one was open for 0% -> 0% of each run, Pallas kernels for 0% -> 0%
where the time goes in v1:
time: 351 us
  Pallas kernels  348 us (99%)
    pallas_call x1, Pallas kernels, per_device(): pl.pallas_call(functools.partial(_kernel, dims), name='mlp_pipe', out_sha...  348 us

profile of v1, /device:TPU:121, one launch (start us, length us, event | category | flops | bytes accessed | tf_op | source)
XLA Modules:
  0.0 350.5 jit_solution(15770915646272649496)
XLA Ops:
  0.0 1.3 copy.5.gain_ref
  1.3 347.6 %mlp_pipe.1 = bf16[4,8,3072]{2,1,0:T(8,128)(2,1)} custom-call(bf16[16,8,3072]{2,1,0:T(8,128)(2,1)} %x_hbm.1, bf16[2,1,3072]{2,1,0:T(2,128)(2,1)} %copy.5.gain_ref, bf16[2,3072,1024]{2,1,0:T(8,128)(2,1)} %bitcast.2, bf16[2,1024,3072]{2,1,0:T(8,128)(2,1)} %bitcast.3), custom_call_target="tpu_custom_call" | custom-call | tf_op jit(solution)/shard_map/mlp_pipe/pallas_call | solution.py:256
  348.9 1.6 copy.7

commit v2 on v1

v2 whole, which is shorter than its diff:
```python
import functools

import jax
import jax.numpy as jnp
from jax import lax
from jax.experimental import pallas as pl
from jax.experimental.pallas import tpu as pltpu
from jax.sharding import PartitionSpec as P

MESH = pl.DeviceIdType.MESH
NORM_EPS = 1e-5
CORES = 2
LOOKAHEAD = 2
REDUCE_AT = 2
FORWARD_AT = 5


def _f32(a):
    return a.astype(jnp.float32)


def _bf16(a):
    return a.astype(jnp.bfloat16)


def _kernel(dims, x_hbm, gain_ref, w1_hbm, w2_hbm, out_ref,
            w1, w2, xs, xbuf, ybuf, rbuf, lbuf, hold, hbuf, abuf, sbuf, fbuf, obuf,
            wl_sem, wp_send, wp_recv, xl_sem, x_send, x_recv, ready,
            rs_send, rs_recv, l_recv, ag_send, ag_first, ag_rest, f_send, f_recv):
    stages, chips, visits, tok, width, hid = dims
    ranks = chips * CORES
    slab = width // chips
    half = slab // 2
    tsh = tok // ranks
    per_stage = visits * CORES // stages
    p = lax.axis_index("pp")
    t = lax.axis_index("tp")
    c = t // CORES
    k = lax.rem(t, CORES)
    nxt = lax.rem(p + 1, stages)
    right, left = lax.rem(c + 1, chips), lax.rem(c + chips - 1, chips)
    far = lax.rem(c + 2, chips)
    at_start = p == 0
    at_end = p == stages - 1

    def dev(pp, chip, core):
        return {"pp": pp, "tp": chip * CORES + core}

    def remote(src, dst, ssem, rsem, where):
        return pltpu.make_async_remote_copy(src_ref=src, dst_ref=dst, send_sem=ssem, recv_sem=rsem,
                                            device_id=where, device_id_type=MESH)

    def wait(ref, sem):
        pltpu.make_async_copy(ref, ref, sem).wait()

    def load_w(v, j):
        src, dst = ((w1_hbm, w1), (w2_hbm, w2))[j]
        return pltpu.make_async_copy(src.at[v], dst.at[v, k], wl_sem.at[v, j])

    def push_w(v, j):
        src, dst = ((w1_hbm, w1), (w2_hbm, w2))[j]
        return remote(src.at[v], dst.at[v, k], wp_send.at[v, j], wp_recv.at[v, j], dev(p, c, 1 - k))

    x_load = pltpu.make_async_copy(x_hbm, xs, xl_sem)
    x_load.start()
    for v in range(2):
        for j in range(2):
            load_w(v, j).start()

    bar = pltpu.get_barrier_semaphore()
    for r in range(ranks):
        @pl.when(r != t)
        def _(r=r):
            pl.semaphore_signal(bar, inc=1, device_id={"pp": p, "tp": r}, device_id_type=MESH)

    @pl.when(jnp.logical_not(at_end))
    def _():
        for q in range(chips):
            pl.semaphore_signal(bar, inc=1, device_id=dev(nxt, q, k), device_id_type=MESH)
    pl.semaphore_wait(bar, jnp.where(at_start, ranks - 1, ranks - 1 + chips))

    @pl.when(jnp.logical_not(at_start))
    def _():
        for q in range(chips):
            pl.semaphore_signal(ready, inc=1, device_id=dev(p - 1, q, k), device_id_type=MESH)

    def x_copy(i, core, chip):
        return remote(xs.at[CORES * i + core], xbuf.at[i, t], x_send.at[chip], x_recv.at[i], dev(p, chip, core))

    def x_share(i):
        xbuf[i, t] = xs[CORES * i + k]
        for core in range(CORES):
            for chip in (far, right, left):
                x_copy(i, core, chip).start()

    @pl.when(at_start)
    def _():
        x_load.wait()
        for i in range(visits):
            x_copy(i, 1 - k, c).start()
        for i in range(LOOKAHEAD):
            x_share(i)

    for v in range(2):
        for j in range(2):
            push_w(v, j).start()

    def share(i, par, piece, chip, sem):
        return remote(ybuf.at[i, piece[0], piece[1]], ybuf.at[i, piece[0], piece[1]], ag_send.at[par], sem, dev(p, chip, k))

    def reduce_slab(idx):
        i = lax.rem(idx, visits)
        par = lax.rem(idx, 2)

        @pl.when(idx >= jnp.where(at_start, visits + 2, 2))
        def _():
            wait(ybuf.at[i, 0:3], ag_send.at[par])

        with jax.named_scope("wait_rs"):
            wait(rbuf.at[i], rs_recv.at[i])
        for h in range(2):
            ybuf[i, c, h] = _bf16(_f32(rbuf[i, 0, h]) + _f32(rbuf[i, 1, h]) + _f32(rbuf[i, 2, h]))
        share(i, par, (c, 0), right, ag_first.at[i, 0]).start()
        share(i, par, (c, 1), left, ag_first.at[i, 1]).start()
        share(i, par, (c, 1), right, ag_rest.at[i]).start()
        share(i, par, (c, 0), left, ag_rest.at[i]).start()

    def forward(idx):
        i = lax.rem(idx, visits)
        par = lax.rem(idx, 2)
        with jax.named_scope("wait_fwd"):
            wait(ybuf.at[i, left, 0], ag_first.at[i, 0])
        share(i, par, (left, 0), right, ag_rest.at[i]).start()
        with jax.named_scope("wait_fwd2"):
            wait(ybuf.at[i, right, 1], ag_first.at[i, 1])
        share(i, par, (right, 1), left, ag_rest.at[i]).start()

    @pl.when(jnp.logical_not(at_start))
    def _():
        reduce_slab(0)
        forward(0)

    def f_wait(i):
        dst_stage = (CORES * i) // per_stage
        for r in range(ranks):
            @pl.when((dst_stage != p) | (r != t))
            def _(r=r):
                wait(fbuf.at[i % 2, r], f_send.at[i % 2, r])

    def visit(idx, carry):
        v = idx // visits
        i = lax.rem(idx, visits)
        par = lax.rem(idx, 2)
        first = at_start & (v == 0)
        last = at_end & (v == 1)
        ahead = (idx + 1 < 2 * visits) & (idx + 1 != visits) & ((idx + 1 > visits) | jnp.logical_not(at_start))

        def at(place):
            @pl.when(ahead)
            def _():
                if place == REDUCE_AT:
                    reduce_slab(idx + 1)
                if place == FORWARD_AT:
                    forward(idx + 1)

        @pl.when(first & (i + LOOKAHEAD < visits))
        def _():
            x_share(i + LOOKAHEAD)

        @pl.when(first)
        def _():
            with jax.named_scope("wait_x"):
                wait(xbuf.at[i, 0:ranks - 1], x_recv.at[i])
            for q in range(chips):
                for h in range(2):
                    lo = q * slab + h * half
                    ybuf[i, q, h] = _bf16(_f32(xbuf[i, :, :, lo:lo + half]).reshape(tok, half))

        @pl.when(jnp.logical_not(first))
        def _():
            with jax.named_scope("wait_ag"):
                wait(ybuf.at[i, 0:2], ag_rest.at[i])

        at(0)

        pieces = [(q, h) for q in range(chips) for h in range(2)]
        mean = sum(jnp.sum(_f32(ybuf[i, q, h]), axis=-1, keepdims=True) for q, h in pieces) * (1.0 / width)
        var = jnp.zeros_like(mean)
        for q, h in pieces:
            a = _f32(ybuf[i, q, h]) - mean
            var = var + jnp.sum(a * a, axis=-1, keepdims=True)
        scale = lax.rsqrt(var * (1.0 / width) + NORM_EPS)
        for q, h in pieces:
            cols = slice(q * slab + h * half, q * slab + (h + 1) * half)
            hbuf[:, cols] = _bf16((_f32(ybuf[i, q, h]) - mean) * scale * _f32(gain_ref[v, :, cols]))

        def wait_weights(j):
            @pl.when(i == 0)
            def _():
                load_w(v, j).wait()
                push_w(v, j).wait_recv()

        at(1)
        with jax.named_scope("wait_w1"):
            wait_weights(0)
        for s in range(CORES):
            for n in range(0, hid, 512):
                acc = jnp.dot(hbuf[...], w1[v, s, :, n:n + 512], preferred_element_type=jnp.float32)
                abuf[s, :, n:n + 512] = _bf16(jax.nn.gelu(acc))
            at(2 + s)
        with jax.named_scope("wait_w2"):
            wait_weights(1)

        @pl.when(idx == 0)
        def _():
            @pl.when(jnp.logical_not(at_end))
            def _():
                pl.semaphore_wait(ready, chips)

        @pl.when(jnp.logical_not(last) & (idx >= 2))
        def _():
            wait(sbuf.at[par], rs_send.at[par])

        @pl.when(last & (i >= 2))
        def _():
            f_wait(i - 2)

        def product(q):
            cols = pl.ds(pl.multiple_of(q * slab, slab), slab)
            prod = jnp.zeros((tok, slab), jnp.float32)
            for s in range(CORES):
                prod = prod + _f32(_bf16(jnp.dot(abuf[s], w2[v, s, :, cols], preferred_element_type=jnp.float32)))

            @pl.when(last)
            def _():
                row_chip = lax.broadcasted_iota(jnp.int32, (tok, slab), 0) // (tsh * CORES)
                whole = jnp.concatenate([_f32(ybuf[i, q, 0]), _f32(ybuf[i, q, 1])], axis=1)
                fbuf[par, :, :, cols] = _bf16((prod + jnp.where(row_chip == c, whole, 0.0)).reshape(ranks, tsh, slab))
            return prod[:, :half], prod[:, half:]

        def partial(slot, h, dst, where, sem):
            return remote(sbuf.at[par, slot, h], dst, rs_send.at[par], sem, where)

        going = jnp.logical_not(last)
        far_prod = product(far)

        @pl.when(going)
        def _():
            for h, chip in ((0, right), (1, left)):
                sbuf[par, 0, h] = _bf16(far_prod[h])
                partial(0, h, lbuf.at[par, h], dev(p, chip, k), l_recv.at[par, h]).start()
        at(4)

        for slot, chip, h in ((1, right, 1), (2, left, 0)):
            prod = product(chip)

            @pl.when(going)
            def _(slot=slot, chip=chip, h=h, prod=prod):
                sbuf[par, slot, h] = _bf16(prod[h])
                hold[1 - h] = prod[1 - h]
                partial(slot, h, rbuf.at[i, slot, h], dev(nxt, chip, k), rs_recv.at[i]).start()
            at(4 + slot)

        own_prod = product(c)

        @pl.when(going)
        def _():
            for h in range(2):
                sbuf[par, 3, h] = _bf16(own_prod[h] + _f32(ybuf[i, c, h]))
            remote(sbuf.at[par, 3], rbuf.at[i, 0], rs_send.at[par], rs_recv.at[i], dev(nxt, c, k)).start()
        at(7)

        @pl.when(going)
        def _():
            for slot, chip, h in ((1, right, 0), (2, left, 1)):
                with jax.named_scope("wait_l"):
                    wait(lbuf.at[par, h], l_recv.at[par, h])
                sbuf[par, slot, h] = _bf16(hold[h] + _f32(lbuf[par, h]))
                partial(slot, h, rbuf.at[i, slot, h], dev(nxt, chip, k), rs_recv.at[i]).start()

        @pl.when(last)
        def _():
            dst_stage = (CORES * i) // per_stage
            slot = lax.rem(CORES * i, per_stage) + k
            for r in range(ranks):
                mine = (dst_stage == p) & (r == t)

                @pl.when(mine)
                def _(r=r):
                    obuf[slot, c] = fbuf[par, r]

                @pl.when(jnp.logical_not(mine))
                def _(r=r):
                    remote(fbuf.at[par, r], obuf.at[slot, c], f_send.at[par, r], f_recv.at[slot, c],
                           {"pp": dst_stage, "tp": r}).start()
        at(8)

        @pl.when(idx + 1 == visits)
        def _():
            reduce_slab(idx + 1)
            forward(idx + 1)

        return carry

    lax.fori_loop(0, 2 * visits, visit, 0)

    with jax.named_scope("wait_out"):
        for j in range(per_stage):
            for q in range(chips):
                mine = at_end & (q == c) & (k == j % CORES)

                @pl.when(jnp.logical_not(mine))
                def _(j=j, q=q):
                    wait(obuf.at[j, q], f_recv.at[j, q])
            total = _f32(obuf[j, 0])
            for q in range(1, chips):
                total = total + _f32(obuf[j, q])
            out_ref[j] = _bf16(total)

    with jax.named_scope("wait_sends"):
        @pl.when(at_end)
        def _():
            for i in (visits - 2, visits - 1):
                f_wait(i)
        for par in range(2):
            wait(sbuf.at[par], rs_send.at[par])
            wait(ybuf.at[0, 0:3], ag_send.at[par])
        for v in range(2):
            for j in range(2):
                push_w(v, j).wait_send()

        @pl.when(jnp.logical_not(at_start))
        def _():
            x_load.wait()

        @pl.when(at_start)
        def _():
            wait(xs.at[0:visits], x_send.at[c])
            for chip in (far, right, left):
                wait(xs, x_send.at[chip])


def solution(mesh):
    stages, ranks = mesh.shape["pp"], mesh.shape["tp"]
    chips = ranks // CORES

    def per_device(x, gain, w_in, w_out):
        micro, tsh, width = x.shape
        passes, _, _, hid = w_in.shape
        tok = tsh * ranks
        visits = micro // CORES
        half = width // chips // 2
        per_stage = micro // stages
        dims = (stages, chips, visits, tok, width, hid)
        bf = jnp.bfloat16
        dma = pltpu.SemaphoreType.DMA
        any_space = pl.BlockSpec(memory_space=pl.ANY)
        vmem = pl.BlockSpec(memory_space=pltpu.VMEM)
        return pl.pallas_call(
            functools.partial(_kernel, dims),
            name="mlp_pipe",
            out_shape=jax.ShapeDtypeStruct((per_stage, tsh, width), bf),
            in_specs=[any_space, vmem, any_space, any_space],
            out_specs=vmem,
            scratch_shapes=[
                pltpu.VMEM((passes, CORES, width, hid), bf),
                pltpu.VMEM((passes, CORES, hid, width), bf),
                pltpu.VMEM((micro, tsh, width), bf),
                pltpu.VMEM((visits, ranks, tsh, width), bf),
                pltpu.VMEM((visits, chips, 2, tok, half), bf),
                pltpu.VMEM((visits, 3, 2, tok, half), bf),
                pltpu.VMEM((2, 2, tok, half), bf),
                pltpu.VMEM((2, tok, half), jnp.float32),
                pltpu.VMEM((tok, width), bf),
                pltpu.VMEM((CORES, tok, hid), bf),
                pltpu.VMEM((2, chips, 2, tok, half), bf),
                pltpu.VMEM((2, ranks, tsh, width), bf),
                pltpu.VMEM((per_stage, chips, tsh, width), bf),
                dma((passes, 2)), dma((passes, 2)), dma((passes, 2)),
                dma, dma((chips,)), dma((visits,)), pltpu.SemaphoreType.REGULAR,
                dma((2,)), dma((visits,)), dma((2, 2)), dma((2,)), dma((visits, 2)), dma((visits,)),
                dma((2, ranks)), dma((per_stage, chips)),
            ],
            compiler_params=pltpu.CompilerParams(collective_id=0, has_side_effects=True, vmem_limit_bytes=67043328),
        )(x, gain, w_in.reshape(passes, width, hid), w_out.reshape(passes, hid, width))

    return jax.shard_map(
        per_device,
        mesh=mesh,
        in_specs=(P("dp", "tp", None), P(None, "pp", None), P(None, "pp", None, "tp"), P(None, "pp", "tp", None)),
        out_specs=P(("dp", "pp"), "tp", None),
        check_vma=False,
    )
```

time: 351 us -> 249 us (0.71)
  Pallas kernels: 348 us -> 245 us
    pallas_call x1, Pallas kernels: 348 us -> 245 us  [per_device(): pl.pallas_call(functools.partial(_kernel, dims), name='mlp_pipe', out_sha...]
where the time goes in v2:
time: 249 us; the launch traced here: 248 us
  Pallas kernels  245 us (98%)
  local copies, waits for them, and re-layouts  2.95 us (1%)
    pallas_call x1, Pallas kernels, per_device(): pl.pallas_call(functools.partial(_kernel, dims), name='mlp_pipe', out_sha...  245 us

profile of v2, /device:TPU:121, one launch (start us, length us, event | category | flops | bytes accessed | tf_op | source)
XLA Modules:
  0.0 248.4 jit_solution(7120068159842115302)
XLA Ops:
  0.0 1.3 copy.5.gain_ref
  1.3 245.4 %mlp_pipe.1 = bf16[4,8,3072]{2,1,0:T(8,128)(2,1)} custom-call(bf16[16,8,3072]{2,1,0:T(8,128)(2,1)} %x_hbm.1, bf16[2,1,3072]{2,1,0:T(2,128)(2,1)} %copy.5.gain_ref, bf16[2,3072,1024]{2,1,0:T(8,128)(2,1)} %bitcast.2, bf16[2,1024,3072]{2,1,0:T(8,128)(2,1)} %bitcast.3), custom_call_target="tpu_custom_call" | custom-call | tf_op jit(solution)/shard_map/mlp_pipe/pallas_call | solution.py:359
  246.7 1.6 copy.7

commit v3 on v2

v3 whole, which is shorter than its diff:
```python
import functools

import jax
import jax.numpy as jnp
from jax import lax
from jax.experimental import pallas as pl
from jax.experimental.pallas import tpu as pltpu
from jax.sharding import PartitionSpec as P

MESH = pl.DeviceIdType.MESH
NORM_EPS = 1e-5
CORES = 2
LOOKAHEAD = 2
REDUCE_AT = 4
LEAD_AT = 11
LEADS = 0
FORWARD_AT = 10
ADD_AT = 10
ADD_LEADS = 1
TILE = 256


def _f32(a):
    return a.astype(jnp.float32)


def _bf16(a):
    return a.astype(jnp.bfloat16)


def _kernel(dims, x_hbm, gain_ref, w1_hbm, w2_hbm, out_ref,
            w1, w2, xs, xbuf, ybuf, rbuf, stat, norm, lbuf, hold, hbuf, accb, abuf, sbuf, tbuf, obuf,
            wl_sem, wp_send, wp_recv, xl_sem, x_send, x_recv, ready,
            rs_send, rs_recv, l_recv, ag_send, ag_first, ag_near, ag_far, st_send, st_recv, o_send, o_recv):
    stages, chips, visits, tok, width, hid = dims
    ranks = chips * CORES
    slab = width // chips
    half = slab // 2
    tsh = tok // ranks
    per_stage = visits * CORES // stages
    p = lax.axis_index("pp")
    t = lax.axis_index("tp")
    c = t // CORES
    k = lax.rem(t, CORES)
    nxt = lax.rem(p + 1, stages)
    right, left = lax.rem(c + 1, chips), lax.rem(c + chips - 1, chips)
    far = lax.rem(c + 2, chips)
    at_start = p == 0
    at_end = p == stages - 1

    def dev(pp, chip, core):
        return {"pp": pp, "tp": chip * CORES + core}

    def remote(src, dst, ssem, rsem, where):
        return pltpu.make_async_remote_copy(src_ref=src, dst_ref=dst, send_sem=ssem, recv_sem=rsem,
                                            device_id=where, device_id_type=MESH)

    def wait(ref, sem):
        pltpu.make_async_copy(ref, ref, sem).wait()

    def load_w(v, j):
        src, dst = ((w1_hbm, w1), (w2_hbm, w2))[j]
        return pltpu.make_async_copy(src.at[v], dst.at[v, k], wl_sem.at[v, j])

    def push_w(v, j):
        src, dst = ((w1_hbm, w1), (w2_hbm, w2))[j]
        return remote(src.at[v], dst.at[v, k], wp_send.at[v, j], wp_recv.at[v, j], dev(p, c, 1 - k))

    x_load = pltpu.make_async_copy(x_hbm, xs, xl_sem)
    x_load.start()
    for v in range(2):
        for j in range(2):
            load_w(v, j).start()

    bar = pltpu.get_barrier_semaphore()
    for r in range(ranks):
        @pl.when(r != t)
        def _(r=r):
            pl.semaphore_signal(bar, inc=1, device_id={"pp": p, "tp": r}, device_id_type=MESH)

    @pl.when(jnp.logical_not(at_end))
    def _():
        for q in range(chips):
            pl.semaphore_signal(bar, inc=1, device_id=dev(nxt, q, k), device_id_type=MESH)
    pl.semaphore_wait(bar, jnp.where(at_start, ranks - 1, ranks - 1 + chips))

    @pl.when(jnp.logical_not(at_start))
    def _():
        for q in range(chips):
            pl.semaphore_signal(ready, inc=1, device_id=dev(p - 1, q, k), device_id_type=MESH)

    def x_copy(i, core, chip):
        return remote(xs.at[CORES * i + core], xbuf.at[i, t], x_send.at[chip], x_recv.at[i], dev(p, chip, core))

    def x_share(i):
        xbuf[i, t] = xs[CORES * i + k]
        for core in range(CORES):
            for chip in (far, right, left):
                x_copy(i, core, chip).start()

    @pl.when(at_start)
    def _():
        x_load.wait()
        for i in range(visits):
            x_copy(i, 1 - k, c).start()
        for i in range(LOOKAHEAD):
            x_share(i)

    for v in range(2):
        for j in range(2):
            push_w(v, j).start()

    def share(i, par, owner, h, chip, sem):
        return remote(ybuf.at[i, owner, h], ybuf.at[i, owner, h], ag_send.at[par], sem, dev(p, chip, k))

    def reduce_slab(idx):
        i = lax.rem(idx, visits)
        par = lax.rem(idx, 2)

        @pl.when(idx >= jnp.where(at_start, visits + 2, 2))
        def _():
            wait(ybuf.at[i, 0:3], ag_send.at[par])
            wait(stat.at[i, 0:3], st_send.at[par])

        with jax.named_scope("wait_rs"):
            wait(rbuf.at[i], rs_recv.at[i])
        own = [_bf16(_f32(rbuf[i, 0, h]) + _f32(rbuf[i, 1, h]) + _f32(rbuf[i, 2, h])) for h in range(2)]
        for h in range(2):
            ybuf[i, c, h] = own[h]
        own = [_f32(a) for a in own]
        mean = sum(jnp.sum(a, axis=-1, keepdims=True) for a in own) * (1.0 / slab)
        dev2 = sum(jnp.sum((a - mean) * (a - mean), axis=-1, keepdims=True) for a in own)
        lane = lax.broadcasted_iota(jnp.int32, (8, 128), 1)
        for j, col in enumerate((mean, dev2)):
            tile = jnp.zeros((8, 128), jnp.float32)
            for a in range(tok // 8):
                tile = jnp.where(lane == a, col[8 * a:8 * a + 8, :], tile)
            stat[i, c, j] = tile
        for chip in (far, right, left):
            remote(stat.at[i, c], stat.at[i, c], st_send.at[par], st_recv.at[i], dev(p, chip, k)).start()
        share(i, par, c, 0, right, ag_first.at[i, 0]).start()
        share(i, par, c, 1, left, ag_first.at[i, 1]).start()
        share(i, par, c, 1, right, ag_near.at[i]).start()
        share(i, par, c, 0, left, ag_near.at[i]).start()

    def forward(idx):
        i = lax.rem(idx, visits)
        par = lax.rem(idx, 2)
        with jax.named_scope("wait_fwd"):
            wait(ybuf.at[i, left, 0], ag_first.at[i, 0])
            share(i, par, left, 0, right, ag_far.at[i]).start()
            wait(ybuf.at[i, right, 1], ag_first.at[i, 1])
            share(i, par, right, 1, left, ag_far.at[i]).start()

    @pl.when(jnp.logical_not(at_start))
    def _():
        reduce_slab(0)
        forward(0)

    def add_relayed(idx):
        i = lax.rem(idx, visits)
        par = lax.rem(idx, 2)
        dst = jnp.where(at_end & (idx >= visits), CORES * i // per_stage, nxt)
        for slot, chip, h in ((1, right, 0), (2, left, 1)):
            got = lax.rem(idx, 3)
            with jax.named_scope("wait_l"):
                wait(lbuf.at[got, h], l_recv.at[got, h])
            sbuf[par, slot, h] = _bf16(hold[par, h] + _f32(lbuf[got, h]))
            remote(sbuf.at[par, slot, h], rbuf.at[i, slot, h], rs_send.at[par], rs_recv.at[i], dev(dst, chip, k)).start()

    def visit(kind, idx, carry):
        v = 0 if kind == "first" else idx // visits
        i = lax.rem(idx, visits)
        dst = jnp.where(at_end & (v == 1), CORES * i // per_stage, nxt)
        par = lax.rem(idx, 2)

        def at(place):
            if place == ADD_AT and place < 10:
                @pl.when(i > ADD_LEADS)
                def _():
                    add_relayed(idx - 1)
            if kind == "first":
                return
            ahead = (idx + 1 < 2 * visits) & (idx + 1 != visits)
            if place == REDUCE_AT:
                @pl.when(ahead & (i >= LEADS))
                def _():
                    reduce_slab(idx + 1)
            if place == LEAD_AT:
                @pl.when(ahead & (i < LEADS))
                def _():
                    reduce_slab(idx + 1)
            if place == FORWARD_AT:
                @pl.when(ahead & (i >= LEADS))
                def _():
                    forward(idx + 1)

        if kind == "first":
            @pl.when(i + LOOKAHEAD < visits)
            def _():
                x_share(i + LOOKAHEAD)
            with jax.named_scope("wait_x"):
                wait(xbuf.at[i, 0:ranks - 1], x_recv.at[i])
            for q in range(chips):
                for h in range(2):
                    lo = q * slab + h * half
                    ybuf[i, q, h] = _bf16(_f32(xbuf[i, :, :, lo:lo + half]).reshape(tok, half))

        at(1)

        def keep(mean, scale):
            norm[0] = jnp.broadcast_to(mean, (tok, 128))
            norm[1] = jnp.broadcast_to(scale, (tok, 128))

        if kind == "first":
            pieces = [(q, h) for q in range(chips) for h in range(2)]
            mean = sum(jnp.sum(_f32(ybuf[i, q, h]), axis=-1, keepdims=True) for q, h in pieces) * (1.0 / width)
            var = jnp.zeros_like(mean)
            for q, h in pieces:
                a = _f32(ybuf[i, q, h]) - mean
                var = var + jnp.sum(a * a, axis=-1, keepdims=True)
            keep(mean, lax.rsqrt(var * (1.0 / width) + NORM_EPS))

        else:
            with jax.named_scope("wait_st"):
                wait(stat.at[i, 0:3], st_recv.at[i])
            means = [stat[i, q, 0] for q in range(chips)]
            mean = sum(means) * (1.0 / chips)
            dev2 = sum(stat[i, q, 1] + slab * (means[q] - mean) * (means[q] - mean) for q in range(chips))
            scale = lax.rsqrt(dev2 * (1.0 / width) + NORM_EPS)
            for a in range(tok // 8):
                rows = slice(8 * a, 8 * a + 8)
                norm[0, rows] = jnp.broadcast_to(mean[:, a:a + 1], (8, 128))
                norm[1, rows] = jnp.broadcast_to(scale[:, a:a + 1], (8, 128))

        def wait_weights(j):
            @pl.when(i == 0)
            def _():
                load_w(v, j).wait()
                push_w(v, j).wait_recv()

        with jax.named_scope("wait_w1"):
            wait_weights(0)
        at(2)
        tile = TILE
        for n_done, chip in enumerate((c, right, left, far)):
            if n_done in (1, 3) and kind != "first":
                with jax.named_scope("wait_ag"):
                    wait(ybuf.at[i, 0], (None, ag_near, None, ag_far)[n_done].at[i])
            for m in range(slab // 128):
                cols = slice(m * 128, (m + 1) * 128)
                gain = gain_ref[v, :, pl.ds(pl.multiple_of(chip * slab + m * 128, 128), 128)]
                h, lo = m * 128 // half, m * 128 % half
                hbuf[:, cols] = _bf16((_f32(ybuf[i, chip, h, :, lo:lo + 128]) - norm[0]) * norm[1] * _f32(gain))
            for s in range(CORES):
                for col in range(0, hid, 2 * tile):
                    rows = pl.ds(pl.multiple_of(chip * slab, slab), slab)
                    cols = slice(col, col + 2 * tile)
                    part = jnp.dot(hbuf[...], w1[v, s, rows, cols], preferred_element_type=jnp.float32)
                    if n_done:
                        part = part + accb[s, :, cols]
                    if n_done < 3:
                        accb[s, :, cols] = part
                    else:
                        abuf[s, :, cols] = _bf16(jax.nn.gelu(part))
            if n_done < 3:
                at(3 + n_done)
        at(6)
        with jax.named_scope("wait_w2"):
            wait_weights(1)

        @pl.when(idx == 0)
        def _():
            @pl.when(jnp.logical_not(at_end))
            def _():
                pl.semaphore_wait(ready, chips)

        @pl.when(idx >= 2)
        def _():
            wait(sbuf.at[par], rs_send.at[par])

        def partial(slot, h, dst, where, sem):
            return remote(sbuf.at[par, slot, h], dst, rs_send.at[par], sem, where)

        def slab_done(n, q, prod):
            prod = prod[:, :half], prod[:, half:]
            if n == 0:
                got = lax.rem(idx, 3)
                for h, chip in ((0, right), (1, left)):
                    sbuf[par, 0, h] = _bf16(prod[h])
                    partial(0, h, lbuf.at[got, h], dev(p, chip, k), l_recv.at[got, h]).start()
            elif n == 3:
                for h in range(2):
                    sbuf[par, 3, h] = _bf16(prod[h] + _f32(ybuf[i, c, h]))


                @pl.when(dst != p)
                def _():
                    remote(sbuf.at[par, 3], rbuf.at[i, 0], rs_send.at[par], rs_recv.at[i], dev(dst, c, k)).start()

                @pl.when(dst == p)
                def _():
                    rbuf[i, 0] = sbuf[par, 3]
            else:
                h = 2 - n
                sbuf[par, n, h] = _bf16(prod[h])
                hold[par, 1 - h] = prod[1 - h]
                partial(n, h, rbuf.at[i, n, h], dev(dst, q, k), rs_recv.at[i]).start()

        order = (far, right, left, c)
        for n, q in enumerate(order):
            cols = pl.ds(pl.multiple_of(q * slab, slab), slab)
            prod = jnp.zeros((tok, slab), jnp.float32)
            for s in range(CORES):
                prod = prod + _f32(_bf16(jnp.dot(abuf[s], w2[v, s, :, cols], preferred_element_type=jnp.float32)))
            slab_done(n, q, prod)
            if n < 3:
                at(7 + n)
        at(10)
        @pl.when((i < ADD_LEADS) | (i == visits - 1) | (ADD_AT > 9))
        def _():
            add_relayed(idx)
        at(11)
        if kind == "mid":
            @pl.when((i < LEADS) & (idx + 1 < 2 * visits) & (idx + 1 != visits))
            def _():
                forward(idx + 1)

        @pl.when(idx + 1 == visits)
        def _():
            reduce_slab(idx + 1)
            forward(idx + 1)

        return carry

    mid_from = jnp.where(at_start, visits, 0)
    lax.fori_loop(0, mid_from, functools.partial(visit, "first"), 0)
    lax.fori_loop(mid_from, 2 * visits, functools.partial(visit, "mid"), 0)

    per_core = per_stage // CORES
    with jax.named_scope("wait_out"):
        for n in range(per_core):
            i = per_core * p + n
            j = CORES * n + k

            @pl.when(at_end)
            def _(i=i):
                wait(rbuf.at[i, 0:2], rs_recv.at[i])

            @pl.when(jnp.logical_not(at_end))
            def _(i=i):
                wait(rbuf.at[i], rs_recv.at[i])
            for h in range(2):
                total = _bf16(_f32(rbuf[i, 0, h]) + _f32(rbuf[i, 1, h]) + _f32(rbuf[i, 2, h]))
                tbuf[n, :, :, h * half:(h + 1) * half] = _bf16(_f32(total).reshape(ranks, tsh, half))
            for r in range(ranks):
                @pl.when(r == t)
                def _(r=r, n=n, j=j):
                    obuf[j, c] = tbuf[n, r]

                @pl.when(r != t)
                def _(r=r, n=n, j=j):
                    remote(tbuf.at[n, r], obuf.at[j, c], o_send.at[n], o_recv.at[j], {"pp": p, "tp": r}).start()
    with jax.named_scope("wait_out2"):
        for j in range(per_stage):
            @pl.when(j % CORES == k)
            def _(j=j):
                wait(obuf.at[j, 0:chips - 1], o_recv.at[j])

            @pl.when(j % CORES != k)
            def _(j=j):
                wait(obuf.at[j], o_recv.at[j])
            for q in range(chips):
                out_ref[j, :, q * slab:(q + 1) * slab] = obuf[j, q]

    with jax.named_scope("wait_sends"):
        for n in range(per_core):
            wait(tbuf.at[n, 0:ranks - 1], o_send.at[n])
        for par in range(2):
            @pl.when(at_end)
            def _(par=par):
                wait(sbuf.at[par, 0:3], rs_send.at[par])

            @pl.when(jnp.logical_not(at_end))
            def _(par=par):
                wait(sbuf.at[par], rs_send.at[par])
            wait(ybuf.at[0, 0:3], ag_send.at[par])
            wait(stat.at[0, 0:3], st_send.at[par])
        for v in range(2):
            for j in range(2):
                push_w(v, j).wait_send()

        @pl.when(jnp.logical_not(at_start))
        def _():
            x_load.wait()

        @pl.when(at_start)
        def _():
            wait(xs.at[0:visits], x_send.at[c])
            for chip in (far, right, left):
                wait(xs, x_send.at[chip])


def solution(mesh):
    stages, ranks = mesh.shape["pp"], mesh.shape["tp"]
    chips = ranks // CORES

    def per_device(x, gain, w_in, w_out):
        micro, tsh, width = x.shape
        passes, _, _, hid = w_in.shape
        tok = tsh * ranks
        visits = micro // CORES
        half = width // chips // 2
        per_stage = micro // stages
        dims = (stages, chips, visits, tok, width, hid)
        bf = jnp.bfloat16
        dma = pltpu.SemaphoreType.DMA
        any_space = pl.BlockSpec(memory_space=pl.ANY)
        vmem = pl.BlockSpec(memory_space=pltpu.VMEM)
        return pl.pallas_call(
            functools.partial(_kernel, dims),
            name="mlp_pipe",
            out_shape=jax.ShapeDtypeStruct((per_stage, tsh, width), bf),
            in_specs=[any_space, vmem, any_space, any_space],
            out_specs=vmem,
            scratch_shapes=[
                pltpu.VMEM((passes, CORES, width, hid), bf),
                pltpu.VMEM((passes, CORES, hid, width), bf),
                pltpu.VMEM((micro, tsh, width), bf),
                pltpu.VMEM((visits, ranks, tsh, width), bf),
                pltpu.VMEM((visits, chips, 2, tok, half), bf),
                pltpu.VMEM((visits, 3, 2, tok, half), bf),
                pltpu.VMEM((visits, chips, 2, 8, 128), jnp.float32),
                pltpu.VMEM((2, tok, 128), jnp.float32),
                pltpu.VMEM((3, 2, tok, half), bf),
                pltpu.VMEM((2, 2, tok, half), jnp.float32),
                pltpu.VMEM((tok, 2 * half), bf),
                pltpu.VMEM((CORES, tok, hid), jnp.float32),
                pltpu.VMEM((CORES, tok, hid), bf),
                pltpu.VMEM((2, chips, 2, tok, half), bf),
                pltpu.VMEM((per_stage // CORES, ranks, tsh, 2 * half), bf),
                pltpu.VMEM((per_stage, chips, tsh, 2 * half), bf),
                dma((passes, 2)), dma((passes, 2)), dma((passes, 2)),
                dma, dma((chips,)), dma((visits,)), pltpu.SemaphoreType.REGULAR,
                dma((2,)), dma((visits,)), dma((3, 2)), dma((2,)), dma((visits, 2)), dma((visits,)), dma((visits,)), dma((2,)), dma((visits,)),
                dma((per_stage // CORES,)), dma((per_stage,)),
            ],
            compiler_params=pltpu.CompilerParams(collective_id=0, has_side_effects=True, vmem_limit_bytes=67043328),
        )(x, gain, w_in.reshape(passes, width, hid), w_out.reshape(passes, hid, width))

    return jax.shard_map(
        per_device,
        mesh=mesh,
        in_specs=(P("dp", "tp", None), P(None, "pp", None), P(None, "pp", None, "tp"), P(None, "pp", "tp", None)),
        out_specs=P(("dp", "pp"), "tp", None),
        check_vma=False,
    )
```

time: 249 us -> 230 us (0.924)
  Pallas kernels: 245 us -> 227 us
    pallas_call x1, Pallas kernels: 245 us -> 227 us  [per_device(): pl.pallas_call(functools.partial(_kernel, dims), name='mlp_pipe', out_sha...]
where the time goes in v3:
time: 230 us
  Pallas kernels  227 us (99%)
  local copies, waits for them, and re-layouts  2.95 us (1%)
    pallas_call x1, Pallas kernels, per_device(): pl.pallas_call(functools.partial(_kernel, dims), name='mlp_pipe', out_sha...  227 us

profile of v3, /device:TPU:121, one launch (start us, length us, event | category | flops | bytes accessed | tf_op | source)
XLA Modules:
  0.0 230.0 jit_solution(8282836051683110710)
XLA Ops:
  0.0 1.3 copy.5.gain_ref
  1.3 227.0 %mlp_pipe.1 = bf16[4,8,3072]{2,1,0:T(8,128)(2,1)} custom-call(bf16[16,8,3072]{2,1,0:T(8,128)(2,1)} %x_hbm.1, bf16[2,1,3072]{2,1,0:T(2,128)(2,1)} %copy.5.gain_ref, bf16[2,3072,1024]{2,1,0:T(8,128)(2,1)} %bitcast.2, bf16[2,1024,3072]{2,1,0:T(8,128)(2,1)} %bitcast.3), custom_call_target="tpu_custom_call" | custom-call | tf_op jit(solution)/shard_map/mlp_pipe/pallas_call | solution.py:420
  228.3 1.6 copy.7
